TPU v7x, 256 devices: a whole 4x4x8 slice. The times are simulated.
256 devices in a mesh: ta: 8 (over y, z_lo), gx: 8 (over x, core), gy: 4 (over z_hi).
Axes of the slice: x: 4, y: 4, z: 8 (z_hi: 4, z_lo: 2; z = z_hi * 2 + z_lo), core: 2. Of those that a mesh axis runs over, the one named last changes fastest.
Arguments:
- propagator: bfloat16 [8, 2, 4, 3, 4, 3, 64, 4096], P('ta', None, None, None, None, None, 'gx', 'gy'), may hold values from -1.5 to 1.5
- gamma_table: int32 [16, 8], replicated, may hold values from 0 to 3, as said below
Outputs:
- spectrum: float32 [8, 16, 64, 64, 128], P('ta', None, ('gx', 'gy'))
Inputs may be any that keep to these rules, and one draw needn't show every extreme that they name: gamma_table[g, 0:4] is a permutation of 0 to 3, gamma_table[g, 4:8] are powers of i.
All inputs are finite; a program needn't handle non-finite values.
Results may differ from a plain program's by a relative error of at most 0.0061.
Values may be sent and summed in bfloat16 or wider, within the bound.
A program may use at most 192 MiB of HBM per device.

v0:
```python
import math

import jax
import jax.numpy as jnp
from jax import lax
from jax.sharding import PartitionSpec as P

EXTENT = 64


def channel_weights(channel_table):
    spin_index = jnp.arange(4, dtype=jnp.int32)
    targets = channel_table[:, :4]
    codes_all = channel_table[:, 4:]
    mapping = (targets[:, :, None] == spin_index[None, None, :]).astype(jnp.float32)
    phase_real = (codes_all == 0).astype(jnp.float32) - (codes_all == 2).astype(jnp.float32)
    phase_imag = (codes_all == 1).astype(jnp.float32) - (codes_all == 3).astype(jnp.float32)
    pair_real = (
        phase_real[:, None, :] * phase_real[:, :, None]
        - phase_imag[:, None, :] * phase_imag[:, :, None]
    )
    pair_imag = (
        phase_real[:, None, :] * phase_imag[:, :, None]
        + phase_imag[:, None, :] * phase_real[:, :, None]
    )
    source_map = jnp.transpose(mapping, (0, 2, 1))
    selector = source_map[:, :, None, :, None] * mapping[:, None, :, None, :]
    count_channels = channel_table.shape[0]
    weight_real = (pair_real[:, None, :, :, None] * selector).reshape(count_channels, 256)
    weight_imag = (pair_imag[:, None, :, :, None] * selector).reshape(count_channels, 256)
    return (weight_real, weight_imag)


def spin_products(field_real, field_imag):
    site_count = field_real.shape[-1]
    total_real = jnp.zeros((4, 4, 4, 4, site_count), jnp.float32)
    total_imag = jnp.zeros((4, 4, 4, 4, site_count), jnp.float32)
    for color_in in range(3):
        for color_out in range(3):
            left_real = field_real[:, color_in, :, color_out].astype(jnp.float32)
            left_imag = field_imag[:, color_in, :, color_out].astype(jnp.float32)
            total_real = (
                total_real
                + left_real[:, :, None, None] * left_real[None, None]
                + left_imag[:, :, None, None] * left_imag[None, None]
            )
            total_imag = (
                total_imag
                + left_imag[:, :, None, None] * left_real[None, None]
                - left_real[:, :, None, None] * left_imag[None, None]
            )
    return (total_real.reshape(256, site_count), total_imag.reshape(256, site_count))


def dft_tables(length):
    steps_index = lax.iota(jnp.int32, length)
    phases = steps_index[:, None] * steps_index[None, :] % length
    angles = phases.astype(jnp.float32) * (2.0 * math.pi / length)
    norm_factor = 1.0 / math.sqrt(length)
    return (
        (jnp.cos(angles) * norm_factor).astype(jnp.bfloat16),
        (jnp.sin(angles) * norm_factor).astype(jnp.bfloat16),
    )


def transform(complex_pair, which_axis, out_type, cosine, sine_table):
    field_real, field_imag = complex_pair

    def contract_axis(values, weights):
        moved = jnp.tensordot(
            values, weights, axes=([which_axis], [0]), preferred_element_type=jnp.float32
        )
        return jnp.moveaxis(moved, -1, which_axis)

    new_real = contract_axis(field_real, cosine) + contract_axis(field_imag, sine_table)
    new_imag = contract_axis(field_imag, cosine) - contract_axis(field_real, sine_table)
    return (new_real.astype(out_type), new_imag.astype(out_type))


def body(propagator, gamma_table):
    weight_real, weight_imag = channel_weights(gamma_table)
    stack_real = jnp.concatenate([weight_real, -weight_imag], axis=1).astype(jnp.bfloat16)
    stack_imag = jnp.concatenate([weight_imag, weight_real], axis=1).astype(jnp.bfloat16)
    rows_x = propagator.shape[-2]
    cols_yz = propagator.shape[-1]
    rows_y = cols_yz // EXTENT
    site_count = rows_x * cols_yz
    grid_x = lax.axis_size("gx")
    grid_y = lax.axis_size("gy")
    cosine, sine_table = dft_tables(EXTENT)

    def one_slice(slice_block):
        flattened = slice_block.reshape(2, 4, 3, 4, 3, site_count)
        prod_real, prod_imag = spin_products(flattened[0], flattened[1])
        prod_stack = jnp.concatenate([prod_real, prod_imag], axis=0).astype(jnp.bfloat16)
        dens_real = jnp.dot(stack_real, prod_stack, preferred_element_type=jnp.float32).astype(
            jnp.bfloat16
        )
        dens_imag = jnp.dot(stack_imag, prod_stack, preferred_element_type=jnp.float32).astype(
            jnp.bfloat16
        )
        view = (dens_real.shape[0], rows_x * rows_y, EXTENT)
        dens_real = dens_real.reshape(view)
        dens_imag = dens_imag.reshape(view)

        def along(values, weights):
            return jnp.einsum("cpz,zk->ckp", values, weights, preferred_element_type=jnp.float32)

        new_real = along(dens_real, cosine) + along(dens_imag, sine_table)
        new_imag = along(dens_imag, cosine) - along(dens_real, sine_table)
        return (new_real.astype(jnp.bfloat16), new_imag.astype(jnp.bfloat16))

    along_z = lax.map(one_slice, propagator)

    def arrange(values):
        shape_in = values.shape
        values = values.reshape(
            shape_in[0], shape_in[1], shape_in[2], grid_x, grid_y, rows_x, rows_y
        )
        values = jnp.transpose(values, (0, 1, 2, 3, 5, 4, 6))
        return values.reshape(shape_in[0], shape_in[1], shape_in[2], EXTENT, EXTENT)

    arranged = (
        arrange(lax.all_to_all(along_z[0], ("gx", "gy"), split_axis=2, concat_axis=3, tiled=True)),
        arrange(lax.all_to_all(along_z[1], ("gx", "gy"), split_axis=2, concat_axis=3, tiled=True)),
    )
    arranged = transform(arranged, 4, jnp.bfloat16, cosine, sine_table)
    spec_real, spec_imag = transform(arranged, 3, jnp.float32, cosine, sine_table)
    return jnp.concatenate([spec_real, spec_imag], axis=4)


def solution(mesh):
    return jax.shard_map(
        body,
        mesh=mesh,
        in_specs=(P("ta", None, None, None, None, None, "gx", "gy"), P()),
        out_specs=P("ta", None, ("gx", "gy"), None, None),
        check_vma=False,
    )
```

profile of v0, /device:TPU:49, one launch (start us, length us, event | category | flops | bytes accessed | tf_op | source)
XLA Modules:
  0.0 219.3 jit_solution(13062447782403116315)
XLA Ops:
  0.7 4.4 %fusion.124 = (bf16[1,1,4,3,4,3,8,1024]{7,6,5,4,3,2,1,0:T(8,128)(2,1)S(1)}, bf16[1,1,4,3,4,3,8,1024]{7,6,5,4,3,2,1,0:T(8,128)(2,1)}) fusion(bf16[1,2,4,3,4,3,8,1024]{7,6,5,4,3,2,1,0:T(8,128)(2,1)} %param.2), kind=kLoop, calls=%fused_computation.175 | loop fusion | bytes 9437184 | tf_op jit(solution)/shard_map/while/body/eval_jaxpr/slice | solution.py:94
  5.1 1.6 copy.49
  6.7 5.1 %squeeze.47 = bf16[4,3,4,3,8192]{4,2,3,1,0:T(4,128)(2,1)S(1)} reshape(bf16[1,1,4,3,4,3,8,1024]{7,6,4,5,3,2,1,0:T(8,128)(2,1)} %copy.49) | data formatting | bytes 4718592 | tf_op jit(solution)/shard_map/while/body/eval_jaxpr/squeeze | solution.py:94
  11.8 3.4 %copy.50 = bf16[1,1,4,3,4,3,8,1024]{7,6,4,5,3,2,1,0:T(8,128)(2,1)} copy(bf16[1,1,4,3,4,3,8,1024]{7,6,5,4,3,2,1,0:T(8,128)(2,1)} %get-tuple-element.22) | data formatting | bytes 4718592 | tf_op jit(solution)/shard_map/while/body/eval_jaxpr/slice | solution.py:94
  15.2 6.2 %squeeze.48 = bf16[4,3,4,3,8192]{4,2,3,1,0:T(4,128)(2,1)} reshape(bf16[1,1,4,3,4,3,8,1024]{7,6,4,5,3,2,1,0:T(8,128)(2,1)} %copy.50) | data formatting | bytes 4718592 | tf_op jit(solution)/shard_map/while/body/eval_jaxpr/squeeze | solution.py:94
  21.3 2.5 %fusion.24 = (f32[4,4,8192]{2,1,0:T(4,128)S(1)}, f32[4,4,8192]{2,1,0:T(4,128)S(1)}, f32[4,4,8192]{2,1,0:T(4,128)S(1)}, f32[4,4,8192]{2,1,0:T(4,128)S(1)}, f32[4,...) fusion(bf16[4,3,4,3,8192]{4,2,3,1,0:T(4,128)(2,1)} %squeeze.48,, ...), kind=kLoop, calls=%fused_computation.59 | loop fusion | flops 2359296 | bytes 14155776 | tf_op jit(solution)/shard_map/while/body/eval_jaxpr/convert_element_type | solution.py:41
  23.9 37.5 %add_add_fusion = (f32[4,4,4,4,8192]{4,3,2,1,0:T(4,128)}, f32[4,4,4,4,8192]{4,3,2,1,0:T(4,128)}) fusion(f32[4,4,8192]{2,1,0:T(4,128)S(1)} %get-tuple-element.44, f32[4,4,8192]{2,1,0:T(4,128)S(1)} %get-tuple-element.70, f32[4,4,8192]{2,1,0:T(4,128)S(1)} %get-tuple-element.45, f32[4,4,8192]{2,1,0:T(4,128)S(1)} %get-tuple-element.69, ...), kind=kLoop, calls=%fused_computation.4 | loop fusion | flops 130023424 | bytes 25165824 | tf_op jit(solution)/shard_map/while/body/eval_jaxpr/add | solution.py:43
  61.4 10.0 %reshape.473 = f32[256,8192]{1,0:T(8,128)} reshape(f32[4,4,4,4,8192]{4,3,2,1,0:T(4,128)} %get-tuple-element.19) | data formatting | bytes 16777216 | tf_op jit(solution)/shard_map/while/body/eval_jaxpr/add | solution.py:43
  71.5 12.5 %broadcast_multiply_fusion.2 = (f32[4,4,4,4,8192]{4,3,2,1,0:T(4,128)}, f32[4,4,4,4,8192]{4,3,2,1,0:T(4,128)}, f32[4,4,4,4,8192]{4,3,2,1,0:T(4,128)}, f32[4,4,4,4,8192]{4,3,2,1,0:T(4,128)}) fusion(f32[4,4,8192]{2,1,0:T(4,128)S(1)} %get-tuple-element.43, f32[4,4,8192]{2,1,0:T(4,128)S(1)} %get-tuple-element.71), kind=kLoop, calls=%fused_computation.9 | loop fusion | flops 8388608 | bytes 34603008 | tf_op jit(solution)/shard_map/while/body/eval_jaxpr/mul | solution.py:49
  83.9 10.0 %mul.987 = f32[256,8192]{1,0:T(8,128)} reshape(f32[4,4,4,4,8192]{4,3,2,1,0:T(4,128)} %get-tuple-element.53) | data formatting | bytes 16777216 | tf_op jit(solution)/shard_map/while/body/eval_jaxpr/mul | solution.py:44
  93.9 10.0 %mul.991 = f32[256,8192]{1,0:T(8,128)} reshape(f32[4,4,4,4,8192]{4,3,2,1,0:T(4,128)} %get-tuple-element.54) | data formatting | bytes 16777216 | tf_op jit(solution)/shard_map/while/body/eval_jaxpr/mul | solution.py:45
  103.9 10.0 %reshape.474 = f32[256,8192]{1,0:T(8,128)} reshape(f32[4,4,4,4,8192]{4,3,2,1,0:T(4,128)} %get-tuple-element.20) | data formatting | bytes 16777216 | tf_op jit(solution)/shard_map/while/body/eval_jaxpr/sub | solution.py:48
  113.9 10.0 %mul.1021 = f32[256,8192]{1,0:T(8,128)} reshape(f32[4,4,4,4,8192]{4,3,2,1,0:T(4,128)} %get-tuple-element.51) | data formatting | bytes 16777216 | tf_op jit(solution)/shard_map/while/body/eval_jaxpr/mul | solution.py:49
  124.0 10.0 %mul.1023 = f32[256,8192]{1,0:T(8,128)} reshape(f32[4,4,4,4,8192]{4,3,2,1,0:T(4,128)} %get-tuple-element.52) | data formatting | bytes 16777216 | tf_op jit(solution)/shard_map/while/body/eval_jaxpr/mul | solution.py:50
  134.3 9.1 %add_convert_fusion = bf16[256,8192]{1,0:T(8,128)(2,1)S(1)} fusion(f32[256,8192]{1,0:T(8,128)} %mul.991, f32[256,8192]{1,0:T(8,128)} %reshape.473, f32[256,8192]{1,0:T(8,128)} %mul.987), kind=kLoop, calls=%fused_computation.6 | loop fusion | flops 6291456 | bytes 29360128 | tf_op jit(solution)/shard_map/convert.20
  143.4 1.5 copy-done
  144.9 2.4 %copy-done.1 = f32[256,8192]{1,0:T(8,128)S(1)} copy-done((f32[256,8192]{1,0:T(8,128)S(1)}, f32[256,8192]{1,0:T(8,128)}, u32[]{:S(2)}) %copy-start.1) | copy-done | bytes 8388632
  147.3 7.1 %subtract_convert_fusion = bf16[256,8192]{1,0:T(8,128)(2,1)} fusion(f32[256,8192]{1,0:T(8,128)S(1)} %copy-done.1, f32[256,8192]{1,0:T(8,128)} %reshape.474, f32[256,8192]{1,0:T(8,128)S(1)} %copy-done), kind=kLoop, calls=%fused_computation.5 | loop fusion | flops 6291456 | bytes 29360128 | tf_op jit(solution)/shard_map/convert.21
  154.4 4.0 %convolution_convert_fusion.1 = bf16[16,8192]{1,0:T(8,128)(2,1)S(1)} fusion(bf16[256,8192]{1,0:T(8,128)(2,1)} %subtract_convert_fusion, bf16[256,8192]{1,0:T(8,128)(2,1)S(1)} %add_convert_fusion, bf16[16,256]{1,0:T(8,128)(2,1)S(1)} %copy.48, bf16[16,256]{1,0:T(8,128)(2,1)S(1)} %copy.47), kind=kOutput, calls=%fused_computation.1 | convolution fusion | flops 151158784 | bytes 8667136 | tf_op jit(solution)/shard_map/while/body/eval_jaxpr/dot_general | solution.py:96
  159.4 4.7 %convolution_convert_fusion = bf16[16,8192]{1,0:T(8,128)(2,1)S(1)} fusion(bf16[256,8192]{1,0:T(8,128)(2,1)} %subtract_convert_fusion, bf16[256,8192]{1,0:T(8,128)(2,1)} %copy-done.2, bf16[16,256]{1,0:T(8,128)(2,1)S(1)} %copy.47, bf16[16,256]{1,0:T(8,128)(2,1)S(1)} %copy.52), kind=kOutput, calls=%fused_computation | convolution fusion | flops 151158784 | bytes 8667136 | tf_op jit(solution)/shard_map/while/body/eval_jaxpr/dot_general | solution.py:99
  165.9 10.9 %all-to-all-start = ((bf16[1,16,64,128]{3,1,0,2:T(8,128)(2,1)}), bf16[1,16,64,128]{3,1,0,2:T(8,128)(2,1)S(1)}, u32[]{:S(2)}, u32[]{:S(2)}) async-start(bf16[1,16,64,128]{3,1,0,2:T(8,128)(2,1)} %copy.55), calls=%async_computation | async-start | bytes 524288 | tf_op jit(solution)/shard_map/all_to_all | solution.py:124
  178.4 11.6 %all-to-all-done = bf16[1,16,64,128]{3,1,0,2:T(8,128)(2,1)S(1)} async-done(((bf16[1,16,64,128]{3,1,0,2:T(8,128)(2,1)}), bf16[1,16,64,128]{3,1,0,2:T(8,128)(2,1)S(1)}, u32[]{:S(2)}, u32[]{:S(2)}) %all-to-all-start) | async-done | bytes 262176 | tf_op jit(solution)/shard_map/all_to_all | solution.py:124
  190.0 4.3 %all-to-all-start.1 = ((bf16[1,16,64,128]{3,1,0,2:T(8,128)(2,1)}), bf16[1,16,64,128]{3,1,0,2:T(8,128)(2,1)S(1)}, u32[]{:S(2)}, u32[]{:S(2)}) async-start(bf16[1,16,64,128]{3,1,0,2:T(8,128)(2,1)} %copy.61), calls=%async_computation.1 | async-start | bytes 524288 | tf_op jit(solution)/shard_map/all_to_all | solution.py:125
  194.4 2.3 %reshape.425 = bf16[1,16,2,8,4,8,16]{6,5,4,3,2,1,0:T(8,128)(2,1)} reshape(bf16[1,16,2,32,128]{4,3,2,1,0:T(8,128)(2,1)S(1)} %bitcast.181) | data formatting | bytes 524288 | tf_op jit(solution)/shard_map/reshape | solution.py:117
  196.7 2.7 %copy.57 = bf16[1,16,2,8,8,4,16]{6,5,4,3,2,1,0:T(4,128)(2,1)S(1)} copy(bf16[1,16,2,8,8,4,16]{6,4,5,3,2,1,0:T(8,128)(2,1)} %bitcast.179) | data formatting | bytes 524288 | tf_op jit(solution)/shard_map/transpose | solution.py:120
  199.4 1.1 reshape.426
  200.5 1.4 fusion.52
  201.9 5.8 %all-to-all-done.1 = bf16[1,16,64,128]{3,1,0,2:T(8,128)(2,1)S(1)} async-done(((bf16[1,16,64,128]{3,1,0,2:T(8,128)(2,1)}), bf16[1,16,64,128]{3,1,0,2:T(8,128)(2,1)S(1)}, u32[]{:S(2)}, u32[]{:S(2)}) %all-to-all-start.1) | async-done | bytes 262176 | tf_op jit(solution)/shard_map/all_to_all | solution.py:125
  207.8 2.3 %reshape.427 = bf16[1,16,2,8,4,8,16]{6,5,4,3,2,1,0:T(8,128)(2,1)} reshape(bf16[1,16,2,32,128]{4,3,2,1,0:T(8,128)(2,1)S(1)} %bitcast.182) | data formatting | bytes 524288 | tf_op jit(solution)/shard_map/reshape | solution.py:117
  210.1 2.7 %copy.63 = bf16[1,16,2,8,8,4,16]{6,5,4,3,2,1,0:T(4,128)(2,1)S(1)} copy(bf16[1,16,2,8,8,4,16]{6,4,5,3,2,1,0:T(8,128)(2,1)} %bitcast.180) | data formatting | bytes 524288 | tf_op jit(solution)/shard_map/transpose | solution.py:120
  214.3 1.6 fusion.2
  217.9 1.3 pad_maximum_fusion.3
  (30 shorter events, 9.1 us)
Async XLA Ops:
  124.0 10.1 %slice-start = ((s32[16,8]{0,1:T(8,128)}), s32[16,4]{0,1:T(4,128)S(1)}, s32[]{:S(2)}) async-start(s32[16,8]{0,1:T(8,128)} %param.3), calls=%async_computation.2 | async-start | bytes 4096 | tf_op jit(solution)/shard_map/slice | solution.py:13
  134.3 10.6 %copy-start = (f32[256,8192]{1,0:T(8,128)S(1)}, f32[256,8192]{1,0:T(8,128)}, u32[]{:S(2)}) copy-start(f32[256,8192]{1,0:T(8,128)} %mul.1021) | copy-start | bytes 25165828
  134.3 13.0 %copy-start.1 = (f32[256,8192]{1,0:T(8,128)S(1)}, f32[256,8192]{1,0:T(8,128)}, u32[]{:S(2)}) copy-start(f32[256,8192]{1,0:T(8,128)} %mul.1023) | copy-start | bytes 25165828
  147.3 7.1 %copy-start.2 = (bf16[256,8192]{1,0:T(8,128)(2,1)}, bf16[256,8192]{1,0:T(8,128)(2,1)S(1)}, u32[]{:S(2)}) copy-start(bf16[256,8192]{1,0:T(8,128)(2,1)S(1)} %add_convert_fusion) | copy-start | bytes 12582916
  165.9 24.1 %all-to-all-start = ((bf16[1,16,64,128]{3,1,0,2:T(8,128)(2,1)}), bf16[1,16,64,128]{3,1,0,2:T(8,128)(2,1)S(1)}, u32[]{:S(2)}, u32[]{:S(2)}) async-start(bf16[1,16,64,128]{3,1,0,2:T(8,128)(2,1)} %copy.55), calls=%async_computation | async-start | bytes 524288 | tf_op jit(solution)/shard_map/all_to_all | solution.py:124
  190.0 17.6 %all-to-all-start.1 = ((bf16[1,16,64,128]{3,1,0,2:T(8,128)(2,1)}), bf16[1,16,64,128]{3,1,0,2:T(8,128)(2,1)S(1)}, u32[]{:S(2)}, u32[]{:S(2)}) async-start(bf16[1,16,64,128]{3,1,0,2:T(8,128)(2,1)} %copy.61), calls=%async_computation.1 | async-start | bytes 524288 | tf_op jit(solution)/shard_map/all_to_all | solution.py:125
where the time goes:
time: 223 us; the launch traced here: 219 us
  local copies, waits for them, and re-layouts  100 us (45%)
  other arithmetic  70.8 us (32%)
  waiting for transfers between devices  17.4 us (8%)
  matrix products  15.7 us (7%)
  starting transfers between devices  15.1 us (7%)
    add x1, other arithmetic, spin_products(): total_real + left_real[:, :, None, None] * left_real[None, None]  37.5 us
    another operation x3, other arithmetic  16.3 us
    mul x1, other arithmetic, spin_products(): left_imag[:, :, None, None] * left_real[None, None]  12.5 us
    all_to_all x1, waiting for transfers between devices, body(): lax.all_to_all(along_z[0], ('gx', 'gy'), split_axis=2, concat_axis=3, til...  11.6 us
    squeeze x2, local copies, waits for them, and re-layouts, one_slice(): prod_real, prod_imag = spin_products(flattened[0], flattened[1])  11.3 us
    all_to_all x1, starting transfers between devices, body(): lax.all_to_all(along_z[0], ('gx', 'gy'), split_axis=2, concat_axis=3, til...  10.9 us
    mul x1, local copies, waits for them, and re-layouts, spin_products(): left_real[:, :, None, None] * left_imag[None, None]  10 us
    add x1, local copies, waits for them, and re-layouts, spin_products(): total_real + left_real[:, :, None, None] * left_real[None, None]  10 us
  transfers between devices with their start and end apart: 2, of which 2 were waited for; matrix products, arithmetic and copies ran while one was open for 4% of the time, Pallas kernels for 0%

commit v1 on v0

v1 whole, which is shorter than its diff:
```python
import functools
import math

import jax
import jax.numpy as jnp
import numpy as np
from jax import lax
from jax.experimental import pallas as pl
from jax.experimental.pallas import tpu as pltpu
from jax.sharding import PartitionSpec as P

EXTENT = 64
CHANNELS = 16
SPINS = 16
COLORS = 9
BLOCKS = 4
LANES = 256
MESH = pl.DeviceIdType.MESH
F32 = jnp.float32
BF16 = jnp.bfloat16
PAIRS = [(lo, hi) for lo in range(SPINS) for hi in range(lo + 1, SPINS)]


def slot_table():
    slots = [(lo, hi, part) for lo, hi in PAIRS for part in (0, 1)]
    slots += [(spin, spin, 0) for spin in range(SPINS)]
    columns = np.repeat(np.array(slots, np.int32), 8, axis=0)
    table = np.zeros((8, columns.shape[0]), np.int32)
    table[:3] = columns.T
    table[3] = np.arange(columns.shape[0]) % 8
    return table


def dft_tables():
    steps = np.arange(EXTENT)
    angles = (steps[:, None] * steps[None, :] % EXTENT) * (2.0 * math.pi / EXTENT)
    norm = 1.0 / math.sqrt(EXTENT)
    return np.cos(angles) * norm, np.sin(angles) * norm


def rotation(cosine, sine):
    table = np.zeros((2, EXTENT, 2, EXTENT))
    table[0, :, 0] = cosine
    table[1, :, 0] = sine
    table[0, :, 1] = -sine
    table[1, :, 1] = cosine
    return table


def weights_z():
    turn = rotation(*dft_tables())
    table = np.zeros((32, 2, 2, 2, 2, 2, EXTENT))
    for y in range(2):
        block = turn.transpose(3, 2, 0, 1).reshape(32, 2, 2, 2, EXTENT)
        table[:, :, :, y, :, y, :] = block
    return table.reshape(256, 256)


def weights_y():
    turn = rotation(*dft_tables())
    swapped = np.stack([turn[:, :, 1], -turn[:, :, 0]], axis=2)
    both = np.stack([turn, swapped], axis=2)
    both = both.reshape(2, 4, 4, 2, 2, 2, 2, EXTENT)
    table = np.zeros((4, 4, 2, 2, 2, 2, 2, 2, 2, EXTENT))
    for kz in range(2):
        table[:, :, :, kz, :, :, :, kz] = both.transpose(1, 2, 3, 0, 4, 5, 6, 7)
    return table.reshape(256, 512)


def weights_x():
    cosine, sine = dft_tables()
    return np.concatenate([cosine.T, sine.T], axis=1)


def channel_rows(gamma, table):
    lo, hi = table[0:1], table[1:2]
    imaginary = table[2:3] == 1

    def pick(base, index):
        out = jnp.zeros((CHANNELS, index.shape[1]), jnp.int32)
        for spin in range(4):
            out = jnp.where(index == spin, gamma[:, base + spin : base + spin + 1], out)
        return out

    lo_1, lo_2 = lax.div(lo, 4), lax.rem(lo, 4)
    hi_1, hi_2 = lax.div(hi, 4), lax.rem(hi, 4)
    phase = {}
    for name, (s1, s2, s3, s4) in {
        "straight": (lo_1, lo_2, hi_1, hi_2),
        "reversed": (hi_1, hi_2, lo_1, lo_2),
    }.items():
        hit = jnp.logical_and(pick(0, s3) == s1, pick(0, s2) == s4)
        turn = jnp.where(hit, lax.rem(pick(4, s3) + pick(4, s2), 4), 7)
        one, zero = jnp.float32(1), jnp.float32(0)
        real = jnp.where(turn == 0, one, zero) - jnp.where(turn == 2, one, zero)
        imag = jnp.where(turn == 1, one, zero) - jnp.where(turn == 3, one, zero)
        phase[name] = (real, imag)
    (r1, i1), (r2, i2) = phase["straight"], phase["reversed"]
    diagonal = lo == hi
    r2 = jnp.where(diagonal, 0.0, r2)
    i2 = jnp.where(diagonal, 0.0, i2)
    rows_real = jnp.where(imaginary, i2 - i1, r1 + r2)
    rows_imag = jnp.where(imaginary, r1 - r2, i1 + i2)
    return rows_real, rows_imag


def plane(part, spin, color):
    s1, s2 = divmod(spin, 4)
    c1, c2 = divmod(color, 3)
    return part * 144 + ((s1 * 3 + c1) * 4 + s2) * 3 + c2


def spin_products(field, products):
    load = lambda part, spin: [field[plane(part, spin, color)] for color in range(COLORS)]

    def chain(terms):
        total = None
        for left, right in terms:
            product = left.astype(F32) * right.astype(F32)
            total = product if total is None else total + product
        return total

    row = 0
    for lo in range(SPINS):
        lo_real, lo_imag = load(0, lo), load(1, lo)
        lo_minus = [-value for value in lo_real]
        for hi in range(lo + 1, SPINS):
            hi_real, hi_imag = load(0, hi), load(1, hi)
            real = chain([*zip(lo_real, hi_real), *zip(lo_imag, hi_imag)])
            imag = chain([*zip(lo_imag, hi_real), *zip(lo_minus, hi_imag)])
            products[row : row + 16] = jnp.concatenate([real, imag], axis=0).astype(BF16)
            row += 16
    for first in range(0, SPINS, 2):
        squares = []
        for spin in (first, first + 1):
            real, imag = load(0, spin), load(1, spin)
            squares.append(chain([*zip(real, real), *zip(imag, imag)]))
        products[row : row + 16] = jnp.concatenate(squares, axis=0).astype(BF16)
        row += 16


def peer(gx, gy, dx, dc, dy):
    core = lax.rem(gx, 2)
    to_core = core + dc - 2 * dc * core
    return lax.rem(gx // 2 + dx, 4) * 2 + to_core, lax.rem(gy + dy, 4)


def send_order():
    by_dy = {dy: [(dx, dc, dy) for dx in range(4) for dc in range(2) if (dx, dc, dy) != (0, 0, 0)] for dy in range(4)}
    order = []
    for step in range(8):
        for dy in (2, 1, 3, 0):
            if step < len(by_dy[dy]):
                order.append(by_dy[dy][step])
    return order


def front_kernel(
    prop, gamma, table, wz, received, field, weights, products, message, load_sem, send_sem, recv_sem
):
    gx, gy = lax.axis_index("gx"), lax.axis_index("gy")
    me = gx * 4 + gy
    offsets = send_order()
    loads = [
        pltpu.make_async_copy(prop.at[:, :, pl.ds(j * LANES, LANES)], field.at[j], load_sem.at[j])
        for j in range(BLOCKS)
    ]
    for load in loads:
        load.start()
    barrier = pltpu.get_barrier_semaphore()
    for offset in offsets:
        to_x, to_y = peer(gx, gy, *offset)
        pl.semaphore_signal(barrier, inc=1, device_id={"gx": to_x, "gy": to_y}, device_id_type=MESH)

    def build(tile, carry):
        at = pl.ds(pl.multiple_of(tile * LANES, LANES), LANES)
        columns = table[:, at]
        keep = lax.broadcasted_iota(jnp.int32, (8, LANES), 0) == columns[3:4]
        for c, rows in enumerate(channel_rows(gamma[...], columns)):
            for g in range(0, CHANNELS, 2):
                pair = [
                    jnp.where(keep, jnp.broadcast_to(rows[g + i : g + i + 1], (8, LANES)), 0.0)
                    for i in range(2)
                ]
                start = c * 128 + g * 8
                weights[start : start + 16, at] = jnp.concatenate(pair, axis=0).astype(BF16)
        return carry

    lax.fori_loop(0, 8, build, 0)

    for j in range(BLOCKS):
        loads[j].wait()

    def block(j, carry):
        spin_products(field.at[j], products)
        density = jnp.dot(weights[...], products[...], preferred_element_type=F32).astype(BF16)
        pieces = [
            jnp.concatenate(
                [density[:128, t * 128 : t * 128 + 128], density[128:, t * 128 : t * 128 + 128]], axis=1
            )
            for t in range(2)
        ]
        along = lax.dot_general(
            wz[...], jnp.concatenate(pieces, axis=0), (((1,), (1,)), ((), ())), preferred_element_type=F32
        )
        along = along.reshape(32, 8, LANES)
        message[j] = jnp.concatenate([along[:, :, :128], along[:, :, 128:]], axis=1).astype(BF16)

        @pl.when(j == 0)
        def _():
            pl.semaphore_wait(barrier, len(offsets))

        for offset in offsets:
            to_x, to_y = peer(gx, gy, *offset)
            pltpu.make_async_remote_copy(
                src_ref=message.at[j, to_x * 4 + to_y],
                dst_ref=received.at[me * 4 + j],
                send_sem=send_sem,
                recv_sem=recv_sem,
                device_id={"gx": to_x, "gy": to_y},
                device_id_type=MESH,
            ).start()
        received[me * 4 + j] = message[j, me]
        return carry

    lax.fori_loop(0, BLOCKS, block, 0)
    remote = pl.ds(0, 31 * BLOCKS)
    everything = received.at[remote]
    pltpu.make_async_copy(everything, everything, send_sem).wait()
    pltpu.make_async_copy(everything, everything, recv_sem).wait()


def back_kernel(received, wy, wx, out, along_y):
    for gx in range(8):
        piece = received[gx * 16 : gx * 16 + 16].reshape(256, 128)
        turned = lax.dot_general(piece, wy[...], (((0,), (0,)), ((), ())), preferred_element_type=F32)
        along_y[gx] = turned.reshape(CHANNELS, 8, 512)
    for g in range(CHANNELS):
        rows = along_y[:, g].reshape(EXTENT, 512)
        rows = jnp.concatenate([rows[:, :256], rows[:, 256:]], axis=0).astype(BF16)
        spectrum = jnp.dot(wx[...], rows, preferred_element_type=F32)
        out[g, 0] = spectrum[:, :128]
        out[g, 1] = spectrum[:, 128:]


def body(propagator, gamma_table):
    vmem = pl.BlockSpec(memory_space=pltpu.VMEM)
    prop = propagator.reshape(288, 8, 1024)
    received = pl.pallas_call(
        front_kernel,
        out_shape=jax.ShapeDtypeStruct((128, 16, 128), BF16),
        in_specs=[pl.BlockSpec(memory_space=pl.ANY), vmem, vmem, vmem],
        out_specs=vmem,
        scratch_shapes=[
            pltpu.VMEM((BLOCKS, 288, 8, LANES), BF16),
            pltpu.VMEM((256, 2048), BF16),
            pltpu.VMEM((2048, LANES), BF16),
            pltpu.VMEM((BLOCKS, 32, 16, 128), BF16),
            pltpu.SemaphoreType.DMA((BLOCKS,)),
            pltpu.SemaphoreType.DMA,
            pltpu.SemaphoreType.DMA,
        ],
        compiler_params=pltpu.CompilerParams(collective_id=0, has_side_effects=True),
    )(prop, gamma_table, jnp.asarray(slot_table()), jnp.asarray(weights_z(), BF16))
    out = pl.pallas_call(
        back_kernel,
        out_shape=jax.ShapeDtypeStruct((CHANNELS, 2, EXTENT, 128), F32),
        in_specs=[vmem, vmem, vmem],
        out_specs=vmem,
        scratch_shapes=[pltpu.VMEM((8, CHANNELS, 8, 512), F32)],
    )(received, jnp.asarray(weights_y(), BF16), jnp.asarray(weights_x(), BF16))
    return out[None]


def solution(mesh):
    return jax.shard_map(
        body,
        mesh=mesh,
        in_specs=(P("ta", None, None, None, None, None, "gx", "gy"), P()),
        out_specs=P("ta", None, ("gx", "gy"), None, None),
        check_vma=False,
    )
```

time: 223 us -> 31.5 us (0.14)
  the two profiles are of different devices: /device:TPU:49 before, /device:TPU:1 now
where the time goes in v1:
time: 31.5 us; the launch traced here: 31.3 us
  Pallas kernels  30 us (95%)
  local copies, waits for them, and re-layouts  1.35 us (4%)
    pallas_call x1, Pallas kernels, body(): pl.pallas_call(front_kernel, out_shape=jax.ShapeDtypeStruct((128, 16, 128...  27.1 us
    pallas_call x1, Pallas kernels, body(): pl.pallas_call(back_kernel, out_shape=jax.ShapeDtypeStruct((CHANNELS, 2,...  2.83 us
    unnamed x1, local copies, waits for them, and re-layouts  1.35 us

profile of v1, /device:TPU:1, one launch (start us, length us, event | category | flops | bytes accessed | tf_op | source)
XLA Modules:
  0.0 31.3 jit_solution(3822589360424701559)
XLA Ops:
  0.0 1.4 %copy.7.gamma = s32[16,8]{1,0:T(8,128)} copy(s32[16,8]{0,1:T(8,128)} %param.7) | data formatting | bytes 1024 | tf_op args[1]
  1.4 27.1 %shard_map.64.received = bf16[128,16,128]{2,1,0:T(8,128)(2,1)} custom-call(bf16[288,8,1024]{2,1,0:T(8,128)(2,1)} %bitcast.2, s32[16,8]{1,0:T(8,128)} %copy.7.gamma, s32[8,2048]{1,0:T(8,128)} %constant.8.clone.table, bf16[256,256]{1,0:T(8,128)(2,1)} %constant.9.clone.wz), custom_call_target="tpu_custom_call" | custom-call | tf_op jit(solution)/shard_map/pallas_call | solution.py:249
  28.5 2.8 %shard_map.65 = f32[16,2,64,128]{3,2,1,0:T(8,128)} custom-call(bf16[128,16,128]{2,1,0:T(8,128)(2,1)} %shard_map.64.received, bf16[256,512]{1,0:T(8,128)(2,1)} %constant.10.clone.wy, bf16[64,128]{1,0:T(8,128)(2,1)} %constant.11.clone.wx), custom_call_target="tpu_custom_call" | custom-call | tf_op jit(solution)/shard_map/pallas_call | solution.py:265

commit v2 on v1

--- a/solution.py
+++ b/solution.py
@@ -15,6 +15,9 @@
 COLORS = 9
 BLOCKS = 4
 LANES = 256
+SERVED = (((0, 1), 0), ((3, 2), 2))
+FRONT_VMEM = 20 * 2**20
+BACK_VMEM = 16 * 2**20
 MESH = pl.DeviceIdType.MESH
 F32 = jnp.float32
 BF16 = jnp.bfloat16
@@ -139,44 +142,60 @@
         row += 16
 
 
-def peer(gx, gy, dx, dc, dy):
+def peer(gx, dx, dc):
     core = lax.rem(gx, 2)
-    to_core = core + dc - 2 * dc * core
-    return lax.rem(gx // 2 + dx, 4) * 2 + to_core, lax.rem(gy + dy, 4)
-
-
-def send_order():
-    by_dy = {dy: [(dx, dc, dy) for dx in range(4) for dc in range(2) if (dx, dc, dy) != (0, 0, 0)] for dy in range(4)}
-    order = []
-    for step in range(8):
-        for dy in (2, 1, 3, 0):
-            if step < len(by_dy[dy]):
-                order.append(by_dy[dy][step])
-    return order
+    return lax.rem(gx // 2 + dx, 4) * 2 + core + dc - 2 * dc * core
+
+
+OFFSETS = [(dx, dc) for dx in (2, 1, 3, 0) for dc in (1, 0)]
 
 
 def front_kernel(
-    prop, gamma, table, wz, received, field, weights, products, message, load_sem, send_sem, recv_sem
+    prop, gamma_hbm, table_hbm, wz_hbm, received,
+    field, gamma, table, wz, weights, products, message, load_sem, small_sem, send_sem, recv_sem,
 ):
     gx, gy = lax.axis_index("gx"), lax.axis_index("gy")
     me = gx * 4 + gy
-    offsets = send_order()
-    loads = [
-        pltpu.make_async_copy(prop.at[:, :, pl.ds(j * LANES, LANES)], field.at[j], load_sem.at[j])
-        for j in range(BLOCKS)
+    barrier = pltpu.get_barrier_semaphore()
+
+    def each_peer(rows, act):
+        for dx, dc in OFFSETS:
+            for to_y in rows:
+                if (dx, dc) == (0, 0):
+                    pl.when(gy != to_y)(functools.partial(act, gx, to_y))
+                else:
+                    act(peer(gx, dx, dc), to_y)
+
+    def greet(to_x, to_y):
+        pl.semaphore_signal(barrier, inc=1, device_id={"gx": to_x, "gy": to_y}, device_id_type=MESH)
+
+    each_peer((0, 1, 2, 3), greet)
+    small = [
+        pltpu.make_async_copy(source, target, small_sem.at[i])
+        for i, (source, target) in enumerate([(gamma_hbm, gamma), (table_hbm, table), (wz_hbm, wz)])
     ]
-    for load in loads:
-        load.start()
-    barrier = pltpu.get_barrier_semaphore()
-    for offset in offsets:
-        to_x, to_y = peer(gx, gy, *offset)
-        pl.semaphore_signal(barrier, inc=1, device_id={"gx": to_x, "gy": to_y}, device_id_type=MESH)
+
+    def load(j):
+        start = j * LANES if isinstance(j, int) else pl.multiple_of(j * LANES, LANES)
+        return pltpu.make_async_copy(prop.at[:, :, pl.ds(start, LANES)], field.at[j], load_sem.at[j])
+
+    small[0].start()
+    small[1].start()
+    load(0).start()
+    small[2].start()
+    for j in range(1, BLOCKS):
+        load(j).start()
+    small[0].wait()
+    small[1].wait()
+    rows = jnp.concatenate([gamma[...].astype(F32), jnp.zeros((8, 112), F32)], axis=1)
+    rows = jnp.concatenate([rows, jnp.zeros((120, 128), F32)], axis=0)
+    channels = jnp.transpose(rows)[:CHANNELS, :8].astype(jnp.int32)
 
     def build(tile, carry):
         at = pl.ds(pl.multiple_of(tile * LANES, LANES), LANES)
         columns = table[:, at]
         keep = lax.broadcasted_iota(jnp.int32, (8, LANES), 0) == columns[3:4]
-        for c, rows in enumerate(channel_rows(gamma[...], columns)):
+        for c, rows in enumerate(channel_rows(channels, columns)):
             for g in range(0, CHANNELS, 2):
                 pair = [
                     jnp.where(keep, jnp.broadcast_to(rows[g + i : g + i + 1], (8, LANES)), 0.0)
@@ -188,10 +207,10 @@
 
     lax.fori_loop(0, 8, build, 0)
 
-    for j in range(BLOCKS):
-        loads[j].wait()
+    small[2].wait()
 
     def block(j, carry):
+        load(j).wait()
         spin_products(field.at[j], products)
         density = jnp.dot(weights[...], products[...], preferred_element_type=F32).astype(BF16)
         pieces = [
@@ -204,33 +223,50 @@
             wz[...], jnp.concatenate(pieces, axis=0), (((1,), (1,)), ((), ())), preferred_element_type=F32
         )
         along = along.reshape(32, 8, LANES)
-        message[j] = jnp.concatenate([along[:, :, :128], along[:, :, 128:]], axis=1).astype(BF16)
+        message[:, j] = jnp.concatenate([along[:, :, :128], along[:, :, 128:]], axis=1).astype(BF16)
+        received[me * BLOCKS + j] = message[me, j]
 
         @pl.when(j == 0)
         def _():
-            pl.semaphore_wait(barrier, len(offsets))
-
-        for offset in offsets:
-            to_x, to_y = peer(gx, gy, *offset)
-            pltpu.make_async_remote_copy(
-                src_ref=message.at[j, to_x * 4 + to_y],
-                dst_ref=received.at[me * 4 + j],
-                send_sem=send_sem,
-                recv_sem=recv_sem,
-                device_id={"gx": to_x, "gy": to_y},
-                device_id_type=MESH,
-            ).start()
-        received[me * 4 + j] = message[j, me]
+            pl.semaphore_wait(barrier, 31)
+
+        for rows, lag in SERVED:
+            if lag == 0:
+                send_block(rows, j)
+            else:
+                pl.when(j >= lag)(functools.partial(send_block, rows, j - lag))
         return carry
 
+    def send(source, target, to_x, to_y):
+        pltpu.make_async_remote_copy(
+            src_ref=source,
+            dst_ref=target,
+            send_sem=send_sem,
+            recv_sem=recv_sem,
+            device_id={"gx": to_x, "gy": to_y},
+            device_id_type=MESH,
+        ).start()
+
+    def send_block(rows, j):
+        each_peer(
+            rows,
+            lambda to_x, to_y: send(
+                message.at[to_x * 4 + to_y, j], received.at[me * BLOCKS + j], to_x, to_y
+            ),
+        )
+
     lax.fori_loop(0, BLOCKS, block, 0)
+    for step in range(BLOCKS, BLOCKS + max(lag for _, lag in SERVED)):
+        for rows, lag in SERVED:
+            if step - lag < BLOCKS:
+                send_block(rows, step - lag)
     remote = pl.ds(0, 31 * BLOCKS)
     everything = received.at[remote]
     pltpu.make_async_copy(everything, everything, send_sem).wait()
     pltpu.make_async_copy(everything, everything, recv_sem).wait()
 
 
-def back_kernel(received, wy, wx, out, along_y):
+def back_kernel(received, wy, wx, out, along_y, spectrum, out_sem):
     for gx in range(8):
         piece = received[gx * 16 : gx * 16 + 16].reshape(256, 128)
         turned = lax.dot_general(piece, wy[...], (((0,), (0,)), ((), ())), preferred_element_type=F32)
@@ -238,36 +274,51 @@
     for g in range(CHANNELS):
         rows = along_y[:, g].reshape(EXTENT, 512)
         rows = jnp.concatenate([rows[:, :256], rows[:, 256:]], axis=0).astype(BF16)
-        spectrum = jnp.dot(wx[...], rows, preferred_element_type=F32)
-        out[g, 0] = spectrum[:, :128]
-        out[g, 1] = spectrum[:, 128:]
+        both = jnp.dot(wx[...], rows, preferred_element_type=F32)
+        spectrum[g, 0] = both[:, :128]
+        spectrum[g, 1] = both[:, 128:]
+        pltpu.make_async_copy(spectrum.at[g], out.at[g], out_sem.at[g]).start()
+    for g in range(CHANNELS):
+        pltpu.make_async_copy(spectrum.at[g], out.at[g], out_sem.at[g]).wait()
 
 
 def body(propagator, gamma_table):
     vmem = pl.BlockSpec(memory_space=pltpu.VMEM)
+    hbm = pl.BlockSpec(memory_space=pltpu.HBM)
     prop = propagator.reshape(288, 8, 1024)
     received = pl.pallas_call(
         front_kernel,
-        out_shape=jax.ShapeDtypeStruct((128, 16, 128), BF16),
-        in_specs=[pl.BlockSpec(memory_space=pl.ANY), vmem, vmem, vmem],
+        out_shape=pltpu.VMEM((128, 16, 128), BF16),
+        in_specs=[hbm, hbm, hbm, hbm],
         out_specs=vmem,
         scratch_shapes=[
             pltpu.VMEM((BLOCKS, 288, 8, LANES), BF16),
+            pltpu.VMEM((8, CHANNELS), jnp.int32),
+            pltpu.VMEM((8, 2048), jnp.int32),
+            pltpu.VMEM((256, 256), BF16),
             pltpu.VMEM((256, 2048), BF16),
             pltpu.VMEM((2048, LANES), BF16),
-            pltpu.VMEM((BLOCKS, 32, 16, 128), BF16),
+            pltpu.VMEM((32, BLOCKS, 16, 128), BF16),
             pltpu.SemaphoreType.DMA((BLOCKS,)),
+            pltpu.SemaphoreType.DMA((3,)),
             pltpu.SemaphoreType.DMA,
             pltpu.SemaphoreType.DMA,
         ],
-        compiler_params=pltpu.CompilerParams(collective_id=0, has_side_effects=True),
-    )(prop, gamma_table, jnp.asarray(slot_table()), jnp.asarray(weights_z(), BF16))
+        compiler_params=pltpu.CompilerParams(
+            collective_id=0, has_side_effects=True, vmem_limit_bytes=FRONT_VMEM
+        ),
+    )(*[pltpu.with_memory_space_constraint(x, pltpu.HBM) for x in (prop, gamma_table.T, jnp.asarray(slot_table()), jnp.asarray(weights_z(), BF16))])
     out = pl.pallas_call(
         back_kernel,
         out_shape=jax.ShapeDtypeStruct((CHANNELS, 2, EXTENT, 128), F32),
         in_specs=[vmem, vmem, vmem],
-        out_specs=vmem,
-        scratch_shapes=[pltpu.VMEM((8, CHANNELS, 8, 512), F32)],
+        out_specs=hbm,
+        scratch_shapes=[
+            pltpu.VMEM((8, CHANNELS, 8, 512), F32),
+            pltpu.VMEM((CHANNELS, 2, EXTENT, 128), F32),
+            pltpu.SemaphoreType.DMA((CHANNELS,)),
+        ],
+        compiler_params=pltpu.CompilerParams(vmem_limit_bytes=BACK_VMEM),
     )(received, jnp.asarray(weights_y(), BF16), jnp.asarray(weights_x(), BF16))
     return out[None]
 

time: 31.5 us -> 26.4 us (0.84)
  the two profiles are of different devices: /device:TPU:1 before, /device:TPU:49 now
where the time goes in v2:
time: 26.4 us; the launch traced here: 26 us
  Pallas kernels  26 us (98%)
    pallas_call x1, Pallas kernels, body(): pl.pallas_call(front_kernel, out_shape=pltpu.VMEM((128, 16, 128), BF16),...  24.3 us
    pallas_call x1, Pallas kernels, body(): pl.pallas_call(back_kernel, out_shape=jax.ShapeDtypeStruct((CHANNELS, 2,...  1.7 us

profile of v2, /device:TPU:49, one launch (start us, length us, event | category | flops | bytes accessed | tf_op | source)
XLA Modules:
  0.0 26.0 jit_solution(9526304552737632266)
XLA Ops:
  0.0 0.0 copy-start.1
  0.0 0.0 copy-start
  0.0 24.3 %shard_map.64.received = bf16[128,16,128]{2,1,0:T(8,128)(2,1)S(1)} custom-call(bf16[288,8,1024]{2,1,0:T(8,128)(2,1)} %bitcast.3, s32[8,16]{1,0:T(8,128)} %bitcast.4, s32[8,2048]{1,0:T(8,128)} %constant.8.clone.table_hbm, bf16[256,256]{1,0:T(8,128)(2,1)} %constant.9.clone.wz_hbm), custom_call_target="tpu_custom_call" | custom-call | tf_op jit(solution)/shard_map/pallas_call | solution.py:289
  24.3 0.0 copy-done.1
  24.3 0.0 copy-done
  24.3 1.7 %shard_map.65 = f32[16,2,64,128]{3,2,1,0:T(8,128)} custom-call(bf16[128,16,128]{2,1,0:T(8,128)(2,1)S(1)} %shard_map.64.received, bf16[256,512]{1,0:T(8,128)(2,1)S(1)} %copy-done, bf16[64,128]{1,0:T(8,128)(2,1)S(1)} %copy-done.1), custom_call_target="tpu_custom_call" | custom-call | tf_op jit(solution)/shard_map/pallas_call | solution.py:311
Async XLA Ops:
  0.0 24.3 %copy-start.1 = (bf16[64,128]{1,0:T(8,128)(2,1)S(1)}, bf16[64,128]{1,0:T(8,128)(2,1)}, u32[]{:S(2)}) copy-start(bf16[64,128]{1,0:T(8,128)(2,1)} %constant.11.clone.wx) | copy-start | bytes 49156
  0.0 24.3 %copy-start = (bf16[256,512]{1,0:T(8,128)(2,1)S(1)}, bf16[256,512]{1,0:T(8,128)(2,1)}, u32[]{:S(2)}) copy-start(bf16[256,512]{1,0:T(8,128)(2,1)} %constant.10.clone.wy) | copy-start | bytes 786436

commit v3 on v2

--- a/solution.py
+++ b/solution.py
@@ -15,7 +15,7 @@
 COLORS = 9
 BLOCKS = 4
 LANES = 256
-SERVED = (((0, 1), 0), ((3, 2), 2))
+EARLY, LATE = (0, 1), (3, 2)
 FRONT_VMEM = 20 * 2**20
 BACK_VMEM = 16 * 2**20
 MESH = pl.DeviceIdType.MESH
@@ -27,10 +27,8 @@
 def slot_table():
     slots = [(lo, hi, part) for lo, hi in PAIRS for part in (0, 1)]
     slots += [(spin, spin, 0) for spin in range(SPINS)]
-    columns = np.repeat(np.array(slots, np.int32), 8, axis=0)
-    table = np.zeros((8, columns.shape[0]), np.int32)
-    table[:3] = columns.T
-    table[3] = np.arange(columns.shape[0]) % 8
+    table = np.zeros((8, 256), np.int32)
+    table[:3] = np.array(slots, np.int32).T
     return table
 
 
@@ -152,10 +150,25 @@
 
 def front_kernel(
     prop, gamma_hbm, table_hbm, wz_hbm, received,
-    field, gamma, table, wz, weights, products, message, load_sem, small_sem, send_sem, recv_sem,
+    field, gamma, table, wz, spread, weights, products, message, load_sem, small_sem, ready_sem, go_sem, send_sem, recv_sem,
 ):
     gx, gy = lax.axis_index("gx"), lax.axis_index("gy")
     me = gx * 4 + gy
+    small = [
+        pltpu.make_async_copy(source, target, small_sem.at[i])
+        for i, (source, target) in enumerate([(gamma_hbm, gamma), (table_hbm, table), (wz_hbm, wz)])
+    ]
+
+    def load(j):
+        start = j * LANES if isinstance(j, int) else pl.multiple_of(j * LANES, LANES)
+        return pltpu.make_async_copy(prop.at[:, :, pl.ds(start, LANES)], field.at[j], load_sem.at[j])
+
+    small[0].start()
+    small[1].start()
+    load(0).start()
+    small[2].start()
+    for j in range(1, BLOCKS):
+        load(j).start()
     barrier = pltpu.get_barrier_semaphore()
 
     def each_peer(rows, act):
@@ -169,44 +182,47 @@
     def greet(to_x, to_y):
         pl.semaphore_signal(barrier, inc=1, device_id={"gx": to_x, "gy": to_y}, device_id_type=MESH)
 
-    each_peer((0, 1, 2, 3), greet)
-    small = [
-        pltpu.make_async_copy(source, target, small_sem.at[i])
-        for i, (source, target) in enumerate([(gamma_hbm, gamma), (table_hbm, table), (wz_hbm, wz)])
-    ]
-
-    def load(j):
-        start = j * LANES if isinstance(j, int) else pl.multiple_of(j * LANES, LANES)
-        return pltpu.make_async_copy(prop.at[:, :, pl.ds(start, LANES)], field.at[j], load_sem.at[j])
-
-    small[0].start()
-    small[1].start()
-    load(0).start()
-    small[2].start()
-    for j in range(1, BLOCKS):
-        load(j).start()
+    early = gy < 2
+
+    @pl.when(early)
+    def _():
+        each_peer(EARLY + LATE, greet)
+
+    @pl.when(jnp.logical_not(early))
+    def _():
+        pl.semaphore_wait(barrier, 16)
+        each_peer(
+            EARLY,
+            lambda to_x, to_y: pl.semaphore_signal(
+                ready_sem, inc=1, device_id={"gx": to_x, "gy": to_y}, device_id_type=MESH
+            ),
+        )
+
+    spread[...] = jnp.zeros_like(spread)
+    slot = lax.div(lax.broadcasted_iota(jnp.int32, (32, LANES), 1), 8)
+    spread[256:288] = jnp.where(
+        slot == lax.broadcasted_iota(jnp.int32, (32, LANES), 0), 1.0, 0.0
+    ).astype(BF16)
     small[0].wait()
     small[1].wait()
     rows = jnp.concatenate([gamma[...].astype(F32), jnp.zeros((8, 112), F32)], axis=1)
     rows = jnp.concatenate([rows, jnp.zeros((120, 128), F32)], axis=0)
     channels = jnp.transpose(rows)[:CHANNELS, :8].astype(jnp.int32)
 
-    def build(tile, carry):
-        at = pl.ds(pl.multiple_of(tile * LANES, LANES), LANES)
-        columns = table[:, at]
-        keep = lax.broadcasted_iota(jnp.int32, (8, LANES), 0) == columns[3:4]
-        for c, rows in enumerate(channel_rows(channels, columns)):
-            for g in range(0, CHANNELS, 2):
-                pair = [
-                    jnp.where(keep, jnp.broadcast_to(rows[g + i : g + i + 1], (8, LANES)), 0.0)
-                    for i in range(2)
-                ]
-                start = c * 128 + g * 8
-                weights[start : start + 16, at] = jnp.concatenate(pair, axis=0).astype(BF16)
-        return carry
-
-    lax.fori_loop(0, 8, build, 0)
-
+    slot_rows = jnp.concatenate(channel_rows(channels, table[...]), axis=0).astype(BF16)
+    keep = lax.broadcasted_iota(jnp.int32, (8, LANES), 0) == lax.rem(
+        lax.broadcasted_iota(jnp.int32, (8, LANES), 1), 8
+    )
+    for tile in range(8):
+        rows = jnp.dot(slot_rows, spread[256 - 32 * tile : 512 - 32 * tile], preferred_element_type=F32)
+        for row in range(0, 32, 2):
+            pair = [
+                jnp.where(keep, jnp.broadcast_to(rows[row + i : row + i + 1], (8, LANES)), 0.0)
+                for i in range(2)
+            ]
+            weights[row * 8 : row * 8 + 16, tile * LANES : (tile + 1) * LANES] = jnp.concatenate(
+                pair, axis=0
+            ).astype(BF16)
     small[2].wait()
 
     def block(j, carry):
@@ -226,15 +242,16 @@
         message[:, j] = jnp.concatenate([along[:, :, :128], along[:, :, 128:]], axis=1).astype(BF16)
         received[me * BLOCKS + j] = message[me, j]
 
-        @pl.when(j == 0)
+        @pl.when(jnp.logical_and(j == 0, early))
         def _():
-            pl.semaphore_wait(barrier, 31)
-
-        for rows, lag in SERVED:
-            if lag == 0:
-                send_block(rows, j)
-            else:
-                pl.when(j >= lag)(functools.partial(send_block, rows, j - lag))
+            pl.semaphore_wait(barrier, 15)
+
+        each_peer(
+            EARLY,
+            lambda to_x, to_y: send(
+                message.at[to_x * 4 + to_y, j], received.at[me * BLOCKS + j], to_x, to_y
+            ),
+        )
         return carry
 
     def send(source, target, to_x, to_y):
@@ -247,19 +264,23 @@
             device_id_type=MESH,
         ).start()
 
-    def send_block(rows, j):
-        each_peer(
-            rows,
-            lambda to_x, to_y: send(
-                message.at[to_x * 4 + to_y, j], received.at[me * BLOCKS + j], to_x, to_y
-            ),
-        )
-
     lax.fori_loop(0, BLOCKS, block, 0)
-    for step in range(BLOCKS, BLOCKS + max(lag for _, lag in SERVED)):
-        for rows, lag in SERVED:
-            if step - lag < BLOCKS:
-                send_block(rows, step - lag)
+
+    @pl.when(early)
+    def _():
+        pl.semaphore_wait(ready_sem, 16)
+        pl.semaphore_signal(go_sem, inc=1, device_id={"gx": gx, "gy": gy + 2}, device_id_type=MESH)
+
+    @pl.when(jnp.logical_not(early))
+    def _():
+        pl.semaphore_wait(go_sem, 1)
+
+    each_peer(
+        LATE,
+        lambda to_x, to_y: send(
+            message.at[to_x * 4 + to_y], received.at[pl.ds(me * BLOCKS, BLOCKS)], to_x, to_y
+        ),
+    )
     remote = pl.ds(0, 31 * BLOCKS)
     everything = received.at[remote]
     pltpu.make_async_copy(everything, everything, send_sem).wait()
@@ -294,13 +315,16 @@
         scratch_shapes=[
             pltpu.VMEM((BLOCKS, 288, 8, LANES), BF16),
             pltpu.VMEM((8, CHANNELS), jnp.int32),
-            pltpu.VMEM((8, 2048), jnp.int32),
+            pltpu.VMEM((8, 256), jnp.int32),
             pltpu.VMEM((256, 256), BF16),
+            pltpu.VMEM((512, LANES), BF16),
             pltpu.VMEM((256, 2048), BF16),
             pltpu.VMEM((2048, LANES), BF16),
             pltpu.VMEM((32, BLOCKS, 16, 128), BF16),
             pltpu.SemaphoreType.DMA((BLOCKS,)),
             pltpu.SemaphoreType.DMA((3,)),
+            pltpu.SemaphoreType.REGULAR,
+            pltpu.SemaphoreType.REGULAR,
             pltpu.SemaphoreType.DMA,
             pltpu.SemaphoreType.DMA,
         ],

time: 26.4 us -> 25.5 us (0.966); the launches traced: 26 us -> 25.4 us
  Pallas kernels: 26 us -> 25.4 us
    pallas_call x1, Pallas kernels: 24.3 us -> 23.7 us  [body(): pl.pallas_call(front_kernel, out_shape=pltpu.VMEM((128, 16, 128), BF16),...]
where the time goes in v3:
time: 25.5 us; the launch traced here: 25.4 us
  Pallas kernels  25.4 us (100%)
    pallas_call x1, Pallas kernels, body(): pl.pallas_call(front_kernel, out_shape=pltpu.VMEM((128, 16, 128), BF16),...  23.7 us
    pallas_call x1, Pallas kernels, body(): pl.pallas_call(back_kernel, out_shape=jax.ShapeDtypeStruct((CHANNELS, 2,...  1.7 us

profile of v3, /device:TPU:49, one launch (start us, length us, event | category | flops | bytes accessed | tf_op | source)
XLA Modules:
  0.0 25.4 jit_solution(1037856248492852043)
XLA Ops:
  0.0 0.0 copy-start.1
  0.0 0.0 copy-start
  0.0 23.7 %shard_map.64.received = bf16[128,16,128]{2,1,0:T(8,128)(2,1)S(1)} custom-call(bf16[288,8,1024]{2,1,0:T(8,128)(2,1)} %bitcast.3, s32[8,16]{1,0:T(8,128)} %bitcast.4, s32[8,256]{1,0:T(8,128)} %constant.8.clone.table_hbm, bf16[256,256]{1,0:T(8,128)(2,1)} %constant.9.clone.wz_hbm), custom_call_target="tpu_custom_call" | custom-call | tf_op jit(solution)/shard_map/pallas_call | solution.py:310
  23.7 0.0 copy-done.1
  23.7 0.0 copy-done
  23.7 1.7 %shard_map.65 = f32[16,2,64,128]{3,2,1,0:T(8,128)} custom-call(bf16[128,16,128]{2,1,0:T(8,128)(2,1)S(1)} %shard_map.64.received, bf16[256,512]{1,0:T(8,128)(2,1)S(1)} %copy-done, bf16[64,128]{1,0:T(8,128)(2,1)S(1)} %copy-done.1), custom_call_target="tpu_custom_call" | custom-call | tf_op jit(solution)/shard_map/pallas_call | solution.py:335
Async XLA Ops:
  0.0 23.7 %copy-start.1 = (bf16[64,128]{1,0:T(8,128)(2,1)S(1)}, bf16[64,128]{1,0:T(8,128)(2,1)}, u32[]{:S(2)}) copy-start(bf16[64,128]{1,0:T(8,128)(2,1)} %constant.11.clone.wx) | copy-start | bytes 49156
  0.0 23.7 %copy-start = (bf16[256,512]{1,0:T(8,128)(2,1)S(1)}, bf16[256,512]{1,0:T(8,128)(2,1)}, u32[]{:S(2)}) copy-start(bf16[256,512]{1,0:T(8,128)(2,1)} %constant.10.clone.wy) | copy-start | bytes 786436

commit v4 on v3

--- a/solution.py
+++ b/solution.py
@@ -16,6 +16,7 @@
 BLOCKS = 4
 LANES = 256
 EARLY, LATE = (0, 1), (3, 2)
+PARCELS = ((0, 0), (1, 1), (2, 3))
 FRONT_VMEM = 20 * 2**20
 BACK_VMEM = 16 * 2**20
 MESH = pl.DeviceIdType.MESH
@@ -58,14 +59,11 @@
 
 
 def weights_y():
-    turn = rotation(*dft_tables())
-    swapped = np.stack([turn[:, :, 1], -turn[:, :, 0]], axis=2)
-    both = np.stack([turn, swapped], axis=2)
-    both = both.reshape(2, 4, 4, 2, 2, 2, 2, EXTENT)
-    table = np.zeros((4, 4, 2, 2, 2, 2, 2, 2, 2, EXTENT))
+    turn = rotation(*dft_tables()).reshape(2, 4, 4, 2, 2, 2, EXTENT)
+    table = np.zeros((4, 4, 2, 2, 2, 2, 2, 2, EXTENT))
     for kz in range(2):
-        table[:, :, :, kz, :, :, :, kz] = both.transpose(1, 2, 3, 0, 4, 5, 6, 7)
-    return table.reshape(256, 512)
+        table[:, :, :, kz, :, :, kz] = turn.transpose(1, 2, 3, 0, 4, 5, 6)
+    return table.reshape(256, 256)
 
 
 def weights_x():
@@ -167,8 +165,6 @@
     small[1].start()
     load(0).start()
     small[2].start()
-    for j in range(1, BLOCKS):
-        load(j).start()
     barrier = pltpu.get_barrier_semaphore()
 
     def each_peer(rows, act):
@@ -227,6 +223,7 @@
 
     def block(j, carry):
         load(j).wait()
+        pl.when(j < BLOCKS - 1)(lambda: load(j + 1).start())
         spin_products(field.at[j], products)
         density = jnp.dot(weights[...], products[...], preferred_element_type=F32).astype(BF16)
         pieces = [
@@ -246,13 +243,20 @@
         def _():
             pl.semaphore_wait(barrier, 15)
 
+        for first, last in PARCELS:
+            pl.when(j == last)(functools.partial(send_blocks, first, last + 1 - first))
+        return carry
+
+    def send_blocks(first, count):
         each_peer(
             EARLY,
             lambda to_x, to_y: send(
-                message.at[to_x * 4 + to_y, j], received.at[me * BLOCKS + j], to_x, to_y
+                message.at[to_x * 4 + to_y, pl.ds(first, count)],
+                received.at[pl.ds(me * BLOCKS + first, count)],
+                to_x,
+                to_y,
             ),
         )
-        return carry
 
     def send(source, target, to_x, to_y):
         pltpu.make_async_remote_copy(
@@ -291,10 +295,12 @@
     for gx in range(8):
         piece = received[gx * 16 : gx * 16 + 16].reshape(256, 128)
         turned = lax.dot_general(piece, wy[...], (((0,), (0,)), ((), ())), preferred_element_type=F32)
-        along_y[gx] = turned.reshape(CHANNELS, 8, 512)
+        along_y[gx] = turned.reshape(CHANNELS, 8, 256)
+    sign = jnp.where(lax.broadcasted_iota(jnp.int32, (EXTENT, 128), 1) < EXTENT, 1.0, -1.0)
     for g in range(CHANNELS):
-        rows = along_y[:, g].reshape(EXTENT, 512)
-        rows = jnp.concatenate([rows[:, :256], rows[:, 256:]], axis=0).astype(BF16)
+        rows = along_y[:, g].reshape(EXTENT, 256)
+        swapped = [pltpu.roll(rows[:, kz * 128 : kz * 128 + 128], EXTENT, 1) * sign for kz in range(2)]
+        rows = jnp.concatenate([rows, jnp.concatenate(swapped, axis=1)], axis=0).astype(BF16)
         both = jnp.dot(wx[...], rows, preferred_element_type=F32)
         spectrum[g, 0] = both[:, :128]
         spectrum[g, 1] = both[:, 128:]
@@ -338,7 +344,7 @@
         in_specs=[vmem, vmem, vmem],
         out_specs=hbm,
         scratch_shapes=[
-            pltpu.VMEM((8, CHANNELS, 8, 512), F32),
+            pltpu.VMEM((8, CHANNELS, 8, 256), F32),
             pltpu.VMEM((CHANNELS, 2, EXTENT, 128), F32),
             pltpu.SemaphoreType.DMA((CHANNELS,)),
         ],

time: 25.5 us -> 25.2 us (0.988)
  Pallas kernels: 25.4 us -> 25.1 us
    pallas_call x1, Pallas kernels: 23.7 us -> 23.4 us  [body(): pl.pallas_call(front_kernel, out_shape=pltpu.VMEM((128, 16, 128), BF16),...]
where the time goes in v4:
time: 25.2 us; the launch traced here: 25.1 us
  Pallas kernels  25.1 us (100%)
    pallas_call x1, Pallas kernels, body(): pl.pallas_call(front_kernel, out_shape=pltpu.VMEM((128, 16, 128), BF16),...  23.4 us
    pallas_call x1, Pallas kernels, body(): pl.pallas_call(back_kernel, out_shape=jax.ShapeDtypeStruct((CHANNELS, 2,...  1.66 us

profile of v4, /device:TPU:49, one launch (start us, length us, event | category | flops | bytes accessed | tf_op | source)
XLA Modules:
  0.0 25.1 jit_solution(15951492444252722004)
XLA Ops:
  0.0 0.0 copy-start.1
  0.0 0.0 copy-start
  0.0 23.4 %shard_map.64.received = bf16[128,16,128]{2,1,0:T(8,128)(2,1)S(1)} custom-call(bf16[288,8,1024]{2,1,0:T(8,128)(2,1)} %bitcast.3, s32[8,16]{1,0:T(8,128)} %bitcast.4, s32[8,256]{1,0:T(8,128)} %constant.8.clone.table_hbm, bf16[256,256]{1,0:T(8,128)(2,1)} %constant.9.clone.wz_hbm), custom_call_target="tpu_custom_call" | custom-call | tf_op jit(solution)/shard_map/pallas_call | solution.py:316
  23.4 0.0 copy-done.1
  23.4 0.0 copy-done
  23.4 1.7 %shard_map.65 = f32[16,2,64,128]{3,2,1,0:T(8,128)} custom-call(bf16[128,16,128]{2,1,0:T(8,128)(2,1)S(1)} %shard_map.64.received, bf16[256,256]{1,0:T(8,128)(2,1)S(1)} %copy-done, bf16[64,128]{1,0:T(8,128)(2,1)S(1)} %copy-done.1), custom_call_target="tpu_custom_call" | custom-call | tf_op jit(solution)/shard_map/pallas_call | solution.py:341
Async XLA Ops:
  0.0 23.4 %copy-start.1 = (bf16[64,128]{1,0:T(8,128)(2,1)S(1)}, bf16[64,128]{1,0:T(8,128)(2,1)}, u32[]{:S(2)}) copy-start(bf16[64,128]{1,0:T(8,128)(2,1)} %constant.11.clone.wx) | copy-start | bytes 49156
  0.0 23.4 %copy-start = (bf16[256,256]{1,0:T(8,128)(2,1)S(1)}, bf16[256,256]{1,0:T(8,128)(2,1)}, u32[]{:S(2)}) copy-start(bf16[256,256]{1,0:T(8,128)(2,1)} %constant.10.clone.wy) | copy-start | bytes 393220

commit v5 on v4

--- a/solution.py
+++ b/solution.py
@@ -248,15 +248,16 @@
         return carry
 
     def send_blocks(first, count):
-        each_peer(
-            EARLY,
-            lambda to_x, to_y: send(
-                message.at[to_x * 4 + to_y, pl.ds(first, count)],
-                received.at[pl.ds(me * BLOCKS + first, count)],
-                to_x,
-                to_y,
-            ),
-        )
+        for row in EARLY:
+            each_peer(
+                (row,),
+                lambda to_x, to_y: send(
+                    message.at[to_x * 4 + to_y, pl.ds(first, count)],
+                    received.at[pl.ds(me * BLOCKS + first, count)],
+                    to_x,
+                    to_y,
+                ),
+            )
 
     def send(source, target, to_x, to_y):
         pltpu.make_async_remote_copy(

time: 25.2 us -> 25.2 us (level)
  no operation moved by 1% of the time
where the time goes in v5:
time: 25.2 us; the launch traced here: 25.1 us
  Pallas kernels  25.1 us (100%)
    pallas_call x1, Pallas kernels, body(): pl.pallas_call(front_kernel, out_shape=pltpu.VMEM((128, 16, 128), BF16),...  23.4 us
    pallas_call x1, Pallas kernels, body(): pl.pallas_call(back_kernel, out_shape=jax.ShapeDtypeStruct((CHANNELS, 2,...  1.66 us

profile of v5, /device:TPU:49, one launch (start us, length us, event | category | flops | bytes accessed | tf_op | source)
XLA Modules:
  0.0 25.1 jit_solution(12871552693126858143)
XLA Ops:
  0.0 0.0 copy-start.1
  0.0 0.0 copy-start
  0.0 23.4 %shard_map.64.received = bf16[128,16,128]{2,1,0:T(8,128)(2,1)S(1)} custom-call(bf16[288,8,1024]{2,1,0:T(8,128)(2,1)} %bitcast.3, s32[8,16]{1,0:T(8,128)} %bitcast.4, s32[8,256]{1,0:T(8,128)} %constant.8.clone.table_hbm, bf16[256,256]{1,0:T(8,128)(2,1)} %constant.9.clone.wz_hbm), custom_call_target="tpu_custom_call" | custom-call | tf_op jit(solution)/shard_map/pallas_call | solution.py:317
  23.4 0.0 copy-done.1
  23.4 0.0 copy-done
  23.4 1.7 %shard_map.65 = f32[16,2,64,128]{3,2,1,0:T(8,128)} custom-call(bf16[128,16,128]{2,1,0:T(8,128)(2,1)S(1)} %shard_map.64.received, bf16[256,256]{1,0:T(8,128)(2,1)S(1)} %copy-done, bf16[64,128]{1,0:T(8,128)(2,1)S(1)} %copy-done.1), custom_call_target="tpu_custom_call" | custom-call | tf_op jit(solution)/shard_map/pallas_call | solution.py:342
Async XLA Ops:
  0.0 23.4 %copy-start.1 = (bf16[64,128]{1,0:T(8,128)(2,1)S(1)}, bf16[64,128]{1,0:T(8,128)(2,1)}, u32[]{:S(2)}) copy-start(bf16[64,128]{1,0:T(8,128)(2,1)} %constant.11.clone.wx) | copy-start | bytes 49156
  0.0 23.4 %copy-start = (bf16[256,256]{1,0:T(8,128)(2,1)S(1)}, bf16[256,256]{1,0:T(8,128)(2,1)}, u32[]{:S(2)}) copy-start(bf16[256,256]{1,0:T(8,128)(2,1)} %constant.10.clone.wy) | copy-start | bytes 393220
